TPU v7x, 32 devices: a whole 2x2x4 slice. The times are simulated.
32 devices in a mesh: cls: 32 (over z, y, x, core).
Axes of the slice: x: 2, y: 2, z: 4, core: 2. Of those that a mesh axis runs over, the one named last changes fastest.
Arguments:
- features: bfloat16 [512, 12544], P('cls'), may hold values from -6 to 6
- fc_weight: bfloat16 [12544, 512], replicated, may hold values from -0.0546875 to 0.0546875
- centers: bfloat16 [131072, 512], P('cls'), may hold values from -6 to 6
- labels: int32 [512], replicated, may hold values from 0 to 131071
Outputs:
- loss: float32 [512], P('cls')
- grad_centers: bfloat16 [131072, 512], P('cls')
- grad_fc: float32 [12544, 512], P('cls')
All inputs are finite; a program needn't handle non-finite values.
Results may differ from a plain program's by a relative error of at most 0.0078.
Values may be sent and summed in bfloat16 or wider, within the bound.
A program may use at most 128 MiB of HBM per device.

v0:
```python
import math
import jax
import jax.numpy as jnp
from jax import lax
from jax.sharding import PartitionSpec as P

logit_scale = 64.0
cos_margin = math.cos(0.5)
sin_margin = math.sin(0.5)
epsilon = 1e-06


def inverse_norm(values):
    return lax.rsqrt(jnp.sum(values * values, axis=1, keepdims=True) + epsilon)


def margin_logits(emb_low, center_low, labels, offset):
    cosines = lax.dot_general(
        emb_low, center_low, (((1,), (1,)), ((), ())), preferred_element_type=jnp.float32
    )
    local_ids = labels - offset
    is_target = local_ids[:, None] == lax.broadcasted_iota(jnp.int32, (1, center_low.shape[0]), 1)
    target_cos = jnp.sum(jnp.where(is_target, cosines, 0.0), axis=1)
    target_sine = jnp.sqrt(1.0 - target_cos * target_cos)
    margined = target_cos * cos_margin - target_sine * sin_margin
    logits = logit_scale * jnp.where(is_target, margined[:, None], cosines)
    slope = cos_margin + sin_margin * target_cos / target_sine
    return (logits, is_target, slope)


def swap(blocks):
    return lax.all_to_all(blocks, "cls", split_axis=0, concat_axis=0, tiled=True)


def spread(block, count):
    return swap(jnp.broadcast_to(block[None], (count, *block.shape)))


def on_device(features, fc_weight, centers, labels):
    tok_rows = features.shape[0]
    class_rows = centers.shape[0]
    my_index = lax.axis_index("cls")
    count = lax.axis_size("cls")
    columns = lax.all_to_all(features, "cls", split_axis=1, concat_axis=0, tiled=True)
    embedded = jnp.dot(features, fc_weight, preferred_element_type=jnp.float32).astype(jnp.bfloat16)
    gathered = spread(embedded, count).reshape(count * tok_rows, -1)
    all_float = gathered.astype(jnp.float32)
    emb_low = (all_float * inverse_norm(all_float)).astype(jnp.bfloat16)
    own_float = embedded.astype(jnp.float32)
    inv_emb = inverse_norm(own_float)
    emb_dir = own_float * inv_emb
    center_float = centers.astype(jnp.float32)
    inv_center = inverse_norm(center_float)
    center_dir = center_float * inv_center
    center_low = center_dir.astype(jnp.bfloat16)
    logits, is_target, slope = margin_logits(emb_low, center_low, labels, my_index * class_rows)
    target_logit = jnp.sum(jnp.where(is_target, logits, 0.0), axis=1)
    stats = jnp.stack([jnp.sum(jnp.exp(logits - logit_scale), axis=1), target_logit])
    row_total, target_all = jnp.sum(spread(stats, count), axis=0)
    log_total = logit_scale + jnp.log(row_total)
    loss = lax.dynamic_slice_in_dim(log_total - target_all, my_index * tok_rows, tok_rows)
    probs = jnp.exp(logits - log_total[:, None])
    grad_cos = (
        logit_scale
        * (probs - is_target.astype(jnp.float32))
        * jnp.where(is_target, slope[:, None], 1.0)
    ).astype(jnp.bfloat16)
    grad_unit = lax.dot_general(
        grad_cos, emb_low, (((0,), (0,)), ((), ())), preferred_element_type=jnp.float32
    )
    grad_centers = (
        (grad_unit - center_dir * jnp.sum(grad_unit * center_dir, axis=1, keepdims=True))
        * inv_center
    ).astype(jnp.bfloat16)
    partial = jnp.dot(grad_cos, center_low, preferred_element_type=jnp.float32)
    parts = swap(partial.astype(jnp.bfloat16).reshape(count, tok_rows, -1))
    grad_dir = jnp.sum(parts.astype(jnp.float32), axis=0)
    grad_emb = (
        (grad_dir - emb_dir * jnp.sum(grad_dir * emb_dir, axis=1, keepdims=True)) * inv_emb
    ).astype(jnp.bfloat16)
    all_grads = spread(grad_emb, count).reshape(count * tok_rows, -1)
    grad_fc = lax.dot_general(
        columns, all_grads, (((0,), (0,)), ((), ())), preferred_element_type=jnp.float32
    )
    return (loss, grad_centers, grad_fc)


def solution(mesh):
    placed = (P("cls", None), P(), P("cls", None), P())
    return jax.shard_map(
        on_device,
        mesh=mesh,
        in_specs=placed,
        out_specs=(P("cls"), P("cls", None), P("cls", None)),
        check_vma=False,
    )
```

profile of v0, /device:TPU:0, one launch (start us, length us, event | category | flops | bytes accessed | tf_op | source)
XLA Modules:
  0.0 122.4 jit_solution(10489114198073126917)
XLA Ops:
  0.6 6.7 %fusion.23 = (f32[16]{0:T(128)S(1)}, bf16[16,512]{1,0:T(8,128)(2,1)S(1)}) fusion(bf16[16,12544]{1,0:T(8,128)(2,1)} %param.4, bf16[12544,512]{1,0:T(8,128)(2,1)} %param.5), kind=kOutput, calls=%fused_computation.34 | convolution fusion | flops 205553648 | bytes 13262912 | tf_op jit(solution)/shard_map/dot_general | solution.py:45
  7.3 0.9 broadcast_in_dim.31
  8.2 7.3 %all-to-all-start = ((bf16[32,16,512]{2,1,0:T(8,128)(2,1)}), bf16[32,16,512]{2,1,0:T(8,128)(2,1)S(1)}, u32[]{:S(2)}, u32[]{:S(2)}) async-start(bf16[32,16,512]{2,1,0:T(8,128)(2,1)} %broadcast_in_dim.31), calls=%async_computation | async-start | bytes 1048576 | tf_op jit(solution)/shard_map/all_to_all | solution.py:32
  15.5 6.3 %copy.21 = bf16[4096,512]{0,1:T(8,128)(2,1)} copy(bf16[4096,512]{1,0:T(8,128)(2,1)} %param.6) | data formatting | bytes 8388608 | tf_op args[2]
  21.8 3.1 %fusion.7 = f32[4096]{0:T(1024)S(1)} fusion(bf16[4096,512]{0,1:T(8,128)(2,1)} %copy.21), kind=kLoop, calls=%fused_computation.9 | loop fusion | flops 6287360 | bytes 4210688 | tf_op jit(solution)/shard_map/reduce_sum | solution.py:14
  24.9 6.2 %all-to-all-done = bf16[32,16,512]{2,1,0:T(8,128)(2,1)S(1)} async-done(((bf16[32,16,512]{2,1,0:T(8,128)(2,1)}), bf16[32,16,512]{2,1,0:T(8,128)(2,1)S(1)}, u32[]{:S(2)}, u32[]{:S(2)}) %all-to-all-start) | async-done | bytes 524320 | tf_op jit(solution)/shard_map/all_to_all | solution.py:32
  31.6 4.9 %select_reduce_fusion.1 = (f32[512]{0:T(512)S(1)}, f32[512,4096]{1,0:T(8,128)S(1)}) fusion(s32[512]{0:T(512)S(1)} %broadcast_subtract_fusion, bf16[512,512]{1,0:T(8,128)(2,1)S(1)} %fusion.15, bf16[4096,512]{0,1:T(8,128)(2,1)} %copy.21, f32[4096]{0:T(1024)S(1)} %add_rsqrt_fusion), kind=kOutput, calls=%fused_computation.14 | convolution fusion | flops 2160066048 | bytes 13127680 | tf_op jit(solution)/shard_map/dot_general | solution.py:18
  36.5 3.2 %copy-done.1 = f32[512,4096]{1,0:T(8,128)} copy-done((f32[512,4096]{1,0:T(8,128)}, f32[512,4096]{1,0:T(8,128)S(1)}, u32[]{:S(2)}) %copy-start.1) | copy-done | bytes 8388632
  39.7 4.0 %exponential_reduce_fusion = (f32[512]{0:T(512)S(1)}, f32[512]{0:T(512)S(1)}) fusion(f32[512,4096]{1,0:T(8,128)S(1)} %get-tuple-element.28, f32[512]{0:T(512)S(1)} %get-tuple-element.26, s32[512]{0:T(512)S(1)} %broadcast_subtract_fusion), kind=kLoop, calls=%fused_computation.12 | loop fusion | flops 14679040 | bytes 8396800 | tf_op jit(solution)/shard_map/reduce_sum | solution.py:58
  43.8 11.0 %all_to_all.36 = f32[32,2,512]{2,1,0:T(2,128)S(1)} all-to-all(f32[32,2,512]{2,1,0:T(2,128)S(1)} %broadcast_in_dim.34), channel_id=1, replica_groups=mesh['cls'=32] {'cls'}, dimensions={0} | all-to-all | bytes 262144 | tf_op jit(solution)/shard_map/all_to_all | solution.py:32
  54.9 6.8 %multiply_convert_fusion = bf16[512,4096]{1,0:T(8,128)(2,1)S(1)} fusion(f32[512,4096]{1,0:T(8,128)} %copy-done.1, f32[512]{0:T(512)S(1)} %get-tuple-element.25, f32[512]{0:T(512)S(1)} %bitcast.23, f32[512]{0:T(512)S(1)} %get-tuple-element.26, s32[512]{0:T(512)S(1)} %broadcast_subtract_fusion), kind=kLoop, calls=%fused_computation.10 | loop fusion | flops 20971520 | bytes 12591104 | tf_op jit(solution)/shard_map/convert_element_type | solution.py:67
  61.7 3.2 %fusion.12 = bf16[512,512]{1,0:T(8,128)(2,1)} fusion(bf16[512,4096]{1,0:T(8,128)(2,1)S(1)} %multiply_convert_fusion, bf16[4096,512]{0,1:T(8,128)(2,1)S(1)} %copy-done, f32[4096]{0:T(1024)S(1)} %add_rsqrt_fusion), kind=kOutput, calls=%fused_computation.19 | convolution fusion | flops 2154037248 | bytes 8929280 | tf_op jit(solution)/shard_map/dot_general | solution.py:75
  64.9 2.6 %all-to-all-start.2 = ((bf16[32,16,512]{2,1,0:T(8,128)(2,1)}), bf16[32,16,512]{2,1,0:T(8,128)(2,1)S(1)}, u32[]{:S(2)}, u32[]{:S(2)}) async-start(bf16[32,16,512]{2,1,0:T(8,128)(2,1)} %bitcast.5), calls=%async_computation.2 | async-start | bytes 1048576 | tf_op jit(solution)/shard_map/all_to_all | solution.py:32
  67.5 1.2 all_to_all.28
  68.7 1.1 copy.23
  69.9 13.3 %all-to-all-done.2 = bf16[32,16,512]{2,1,0:T(8,128)(2,1)S(1)} async-done(((bf16[32,16,512]{2,1,0:T(8,128)(2,1)}), bf16[32,16,512]{2,1,0:T(8,128)(2,1)S(1)}, u32[]{:S(2)}, u32[]{:S(2)}) %all-to-all-start.2) | async-done | bytes 524320 | tf_op jit(solution)/shard_map/all_to_all | solution.py:32
  83.1 2.9 %all-to-all-start.4 = ((bf16[16,32,392]{2,0,1:T(8,128)(2,1)}), bf16[16,32,392]{2,0,1:T(8,128)(2,1)S(1)}, u32[]{:S(2)}, u32[]{:S(2)}) async-start(bf16[16,32,392]{2,0,1:T(8,128)(2,1)} %copy.23), calls=%async_computation.4 | async-start | bytes 1048576 | tf_op jit(solution)/shard_map/all_to_all | solution.py:44
  86.0 9.5 %fusion.3 = (f32[4096]{0:T(1024)S(1)}, f32[4096,512]{0,1:T(8,128)}) fusion(bf16[4096,512]{0,1:T(8,128)(2,1)} %copy.21, f32[4096]{0:T(1024)S(1)} %add_rsqrt_fusion, bf16[512,4096]{1,0:T(8,128)(2,1)} %copy-done.2, bf16[512,512]{1,0:T(8,128)(2,1)S(1)} %fusion.15), kind=kOutput, calls=%fused_computation.5 | convolution fusion | flops 2155868160 | bytes 17334272 | tf_op jit(solution)/shard_map/dot_general | solution.py:68
  95.8 5.8 %all-to-all-done.4 = bf16[16,32,392]{2,0,1:T(8,128)(2,1)S(1)} async-done(((bf16[16,32,392]{2,0,1:T(8,128)(2,1)}), bf16[16,32,392]{2,0,1:T(8,128)(2,1)S(1)}, u32[]{:S(2)}, u32[]{:S(2)}) %all-to-all-start.4) | async-done | bytes 401440 | tf_op jit(solution)/shard_map/all_to_all | solution.py:44
  101.6 0.9 broadcast_in_dim.58
  102.5 3.0 %all-to-all-start.3 = ((bf16[32,16,512]{2,1,0:T(8,128)(2,1)}), bf16[32,16,512]{2,1,0:T(8,128)(2,1)S(1)}, u32[]{:S(2)}, u32[]{:S(2)}) async-start(bf16[32,16,512]{2,1,0:T(8,128)(2,1)} %broadcast_in_dim.58), calls=%async_computation.3 | async-start | bytes 1048576 | tf_op jit(solution)/shard_map/all_to_all | solution.py:32
  105.5 8.3 %fusion.6 = bf16[4096,512]{0,1:T(8,128)(2,1)} fusion(f32[4096,512]{0,1:T(8,128)} %get-tuple-element.30, bf16[4096,512]{0,1:T(8,128)(2,1)} %copy.21, f32[4096]{0:T(1024)S(1)} %get-tuple-element.29, f32[4096]{0:T(1024)S(1)} %add_rsqrt_fusion), kind=kLoop, calls=%fused_computation.8 | loop fusion | flops 12582912 | bytes 16809984 | tf_op jit(solution)/shard_map/convert_element_type | solution.py:74
  113.8 6.4 %copy.24 = bf16[4096,512]{1,0:T(8,128)(2,1)} copy(bf16[4096,512]{0,1:T(8,128)(2,1)} %fusion.6) | data formatting | bytes 8388608
  121.1 1.3 %convolution_bitcast_fusion = f32[392,512]{1,0:T(8,128)} fusion(bf16[32,16,512]{2,1,0:T(8,128)(2,1)S(1)} %all-to-all-done.3, bf16[16,32,392]{2,0,1:T(8,128)(2,1)S(1)} %all-to-all-done.4), kind=kOutput, calls=%fused_computation.18 | convolution fusion | flops 205520896 | bytes 1728512 | tf_op jit(solution)/shard_map/dot_general | solution.py:82
  (27 shorter events, 1.9 us)
Async XLA Ops:
  7.3 14.5 %copy-start.4 = (s32[512]{0:T(512)S(1)}, s32[512]{0:T(512)}, u32[]{:S(2)}) copy-start(s32[512]{0:T(512)} %param.7) | copy-start | bytes 6148
  8.2 22.9 %all-to-all-start = ((bf16[32,16,512]{2,1,0:T(8,128)(2,1)}), bf16[32,16,512]{2,1,0:T(8,128)(2,1)S(1)}, u32[]{:S(2)}, u32[]{:S(2)}) async-start(bf16[32,16,512]{2,1,0:T(8,128)(2,1)} %broadcast_in_dim.31), calls=%async_computation | async-start | bytes 1048576 | tf_op jit(solution)/shard_map/all_to_all | solution.py:32
  36.5 3.2 %copy-start.1 = (f32[512,4096]{1,0:T(8,128)}, f32[512,4096]{1,0:T(8,128)S(1)}, u32[]{:S(2)}) copy-start(f32[512,4096]{1,0:T(8,128)S(1)} %get-tuple-element.28) | copy-start | bytes 25165828
  54.9 6.8 %copy-start = (bf16[4096,512]{0,1:T(8,128)(2,1)S(1)}, bf16[4096,512]{0,1:T(8,128)(2,1)}, u32[]{:S(2)}) copy-start(bf16[4096,512]{0,1:T(8,128)(2,1)} %copy.21) | copy-start | bytes 12582916
  61.7 3.2 %copy-start.2 = (bf16[512,4096]{1,0:T(8,128)(2,1)}, bf16[512,4096]{1,0:T(8,128)(2,1)S(1)}, u32[]{:S(2)}) copy-start(bf16[512,4096]{1,0:T(8,128)(2,1)S(1)} %multiply_convert_fusion) | copy-start | bytes 12582916
  61.7 5.8 %copy-start.3 = (bf16[16,12544]{1,0:T(8,128)(2,1)S(1)}, bf16[16,12544]{1,0:T(8,128)(2,1)}, u32[]{:S(2)}) copy-start(bf16[16,12544]{1,0:T(8,128)(2,1)} %param.4) | copy-start | bytes 1204228
  64.9 18.2 %all-to-all-start.2 = ((bf16[32,16,512]{2,1,0:T(8,128)(2,1)}), bf16[32,16,512]{2,1,0:T(8,128)(2,1)S(1)}, u32[]{:S(2)}, u32[]{:S(2)}) async-start(bf16[32,16,512]{2,1,0:T(8,128)(2,1)} %bitcast.5), calls=%async_computation.2 | async-start | bytes 1048576 | tf_op jit(solution)/shard_map/all_to_all | solution.py:32
  83.1 18.5 %all-to-all-start.4 = ((bf16[16,32,392]{2,0,1:T(8,128)(2,1)}), bf16[16,32,392]{2,0,1:T(8,128)(2,1)S(1)}, u32[]{:S(2)}, u32[]{:S(2)}) async-start(bf16[16,32,392]{2,0,1:T(8,128)(2,1)} %copy.23), calls=%async_computation.4 | async-start | bytes 1048576 | tf_op jit(solution)/shard_map/all_to_all | solution.py:44
  102.5 18.6 %all-to-all-start.3 = ((bf16[32,16,512]{2,1,0:T(8,128)(2,1)}), bf16[32,16,512]{2,1,0:T(8,128)(2,1)S(1)}, u32[]{:S(2)}, u32[]{:S(2)}) async-start(bf16[32,16,512]{2,1,0:T(8,128)(2,1)} %broadcast_in_dim.58), calls=%async_computation.3 | async-start | bytes 1048576 | tf_op jit(solution)/shard_map/all_to_all | solution.py:32
where the time goes:
time: 123 us; the launch traced here: 122 us
  waiting for transfers between devices  25.6 us (21%)
  matrix products  25.5 us (21%)
  other arithmetic  23 us (19%)
  local copies, waits for them, and re-layouts  20.7 us (17%)
  starting transfers between devices  15.8 us (13%)
  blocking collectives  11 us (9%)
    all_to_all x3, waiting for transfers between devices, swap(): lax.all_to_all(blocks, 'cls', split_axis=0, concat_axis=0, tiled=True)  19.8 us
    unnamed x12, local copies, waits for them, and re-layouts  16 us
    all_to_all x3, starting transfers between devices, swap(): lax.all_to_all(blocks, 'cls', split_axis=0, concat_axis=0, tiled=True)  12.9 us
    all_to_all x1, blocking collectives, swap(): lax.all_to_all(blocks, 'cls', split_axis=0, concat_axis=0, tiled=True)  11 us
    dot_general x1, matrix products, on_device(): lax.dot_general(grad_cos, emb_low, (((0,), (0,)), ((), ())), preferred_el...  9.45 us
    convert_element_type x1, other arithmetic, on_device(): grad_centers = ((grad_unit - center_dir * jnp.sum(grad_unit * center_dir,...  8.29 us
    convert_element_type x1, other arithmetic, on_device(): grad_cos = (logit_scale * (probs - is_target.astype(jnp.float32)) * jnp.w...  6.78 us
    dot_general x1, matrix products, on_device(): jnp.dot(features, fc_weight, preferred_element_type=jnp.float32)  6.67 us
  transfers between devices with their start and end apart: 4, of which 4 were waited for; matrix products, arithmetic and copies ran while one was open for 29% of the time, Pallas kernels for 0%

commit v1 on v0

--- a/solution.py
+++ b/solution.py
@@ -41,7 +41,10 @@
     class_rows = centers.shape[0]
     my_index = lax.axis_index("cls")
     count = lax.axis_size("cls")
-    columns = lax.all_to_all(features, "cls", split_axis=1, concat_axis=0, tiled=True)
+    columns = jnp.concatenate(
+        lax.all_to_all(jnp.stack(jnp.split(features, lax.axis_size("cls"), axis=1)), "cls", 0, 0),
+        axis=0,
+    )
     embedded = jnp.dot(features, fc_weight, preferred_element_type=jnp.float32).astype(jnp.bfloat16)
     gathered = spread(embedded, count).reshape(count * tok_rows, -1)
     all_float = gathered.astype(jnp.float32)

time: 123 us -> 138 us (1.12)
  local copies, waits for them, and re-layouts: 20.7 us -> 40.5 us
  blocking collectives: 11 us -> 0 us
  starting transfers between devices: 15.8 us -> 21.8 us
    unnamed x12 -> x43, local copies, waits for them, and re-layouts: 16 us -> 36.7 us
    all_to_all x1 -> x0, blocking collectives: 11 us -> none  [swap(): lax.all_to_all(blocks, 'cls', split_axis=0, concat_axis=0, tiled=True)]
    all_to_all x3 -> x4, starting transfers between devices: 12.9 us -> 18.9 us  [swap(): lax.all_to_all(blocks, 'cls', split_axis=0, concat_axis=0, tiled=True)]
    all_to_all x2 -> x0, local copies, waits for them, and re-layouts: 2.32 us -> none  [on_device(): lax.all_to_all(features, 'cls', split_axis=1, concat_axis=0, tiled=True)]
    all_to_all x3 -> x4, waiting for transfers between devices: 19.8 us -> 19.9 us  [swap(): lax.all_to_all(blocks, 'cls', split_axis=0, concat_axis=0, tiled=True)]
  transfers between devices with their start and end apart: 4 -> 5, of which waited for: 4 -> 4; matrix products, arithmetic and copies ran while one was open for 29% -> 41% of each run, Pallas kernels for 0% -> 0%
where the time goes in v1:
time: 138 us; the launch traced here: 137 us
  local copies, waits for them, and re-layouts  40.5 us (29%)
  waiting for transfers between devices  25.7 us (19%)
  matrix products  25.6 us (19%)
  other arithmetic  23 us (17%)
  starting transfers between devices  21.8 us (16%)
    unnamed x43, local copies, waits for them, and re-layouts  36.7 us
    all_to_all x4, waiting for transfers between devices, swap(): lax.all_to_all(blocks, 'cls', split_axis=0, concat_axis=0, tiled=True)  19.9 us
    all_to_all x4, starting transfers between devices, swap(): lax.all_to_all(blocks, 'cls', split_axis=0, concat_axis=0, tiled=True)  18.9 us
    dot_general x1, matrix products, on_device(): lax.dot_general(grad_cos, emb_low, (((0,), (0,)), ((), ())), preferred_el...  9.48 us
    convert_element_type x1, other arithmetic, on_device(): grad_centers = ((grad_unit - center_dir * jnp.sum(grad_unit * center_dir,...  8.29 us
    convert_element_type x1, other arithmetic, on_device(): grad_cos = (logit_scale * (probs - is_target.astype(jnp.float32)) * jnp.w...  6.78 us
    dot_general x1, matrix products, on_device(): jnp.dot(features, fc_weight, preferred_element_type=jnp.float32)  6.7 us
    all_to_all x1, waiting for transfers between devices, on_device(): lax.all_to_all(jnp.stack(jnp.split(features, lax.axis_size('cls'), axis=1...  5.78 us
  transfers between devices with their start and end apart: 5, of which 4 were waited for; matrix products, arithmetic and copies ran while one was open for 41% of the time, Pallas kernels for 0%

profile of v1, /device:TPU:0, one launch (start us, length us, event | category | flops | bytes accessed | tf_op | source)
XLA Modules:
  0.0 137.4 jit_solution(16446296759329911950)
XLA Ops:
  0.6 6.7 %fusion.22 = (f32[16]{0:T(128)S(1)}, bf16[16,512]{1,0:T(8,128)(2,1)S(1)}) fusion(bf16[16,12544]{1,0:T(8,128)(2,1)} %param.4, bf16[12544,512]{1,0:T(8,128)(2,1)} %param.5), kind=kOutput, calls=%fused_computation.65 | convolution fusion | flops 205553648 | bytes 13262912 | tf_op jit(solution)/shard_map/dot_general | solution.py:48
  7.4 0.9 broadcast_in_dim.31
  8.2 7.3 %all-to-all-start = ((bf16[32,16,512]{2,1,0:T(8,128)(2,1)}), bf16[32,16,512]{2,1,0:T(8,128)(2,1)S(1)}, u32[]{:S(2)}, u32[]{:S(2)}) async-start(bf16[32,16,512]{2,1,0:T(8,128)(2,1)} %broadcast_in_dim.31), calls=%async_computation | async-start | bytes 1048576 | tf_op jit(solution)/shard_map/all_to_all | solution.py:32
  22.2 0.7 constant_dynamic-update-slice_fusion.21
  32.3 6.3 %copy.49 = bf16[4096,512]{0,1:T(8,128)(2,1)} copy(bf16[4096,512]{1,0:T(8,128)(2,1)} %param.6) | data formatting | bytes 8388608 | tf_op args[2]
  39.3 3.1 %fusion.7 = f32[4096]{0:T(1024)S(1)} fusion(bf16[4096,512]{0,1:T(8,128)(2,1)} %copy.49), kind=kLoop, calls=%fused_computation.9 | loop fusion | flops 6287360 | bytes 4210688 | tf_op jit(solution)/shard_map/reduce_sum | solution.py:14
  42.9 4.9 %select_reduce_fusion.1 = (f32[512]{0:T(512)S(1)}, f32[512,4096]{1,0:T(8,128)S(1)}) fusion(s32[512]{0:T(512)S(1)} %broadcast_subtract_fusion, bf16[512,512]{1,0:T(8,128)(2,1)S(1)} %fusion.15, bf16[4096,512]{0,1:T(8,128)(2,1)} %copy.49, f32[4096]{0:T(1024)S(1)} %add_rsqrt_fusion), kind=kOutput, calls=%fused_computation.14 | convolution fusion | flops 2160066048 | bytes 13127680 | tf_op jit(solution)/shard_map/dot_general | solution.py:18
  47.8 3.2 %copy-done.1 = f32[512,4096]{1,0:T(8,128)} copy-done((f32[512,4096]{1,0:T(8,128)}, f32[512,4096]{1,0:T(8,128)S(1)}, u32[]{:S(2)}) %copy-start.1) | copy-done | bytes 8388632
  51.0 4.0 %exponential_reduce_fusion = (f32[512]{0:T(512)S(1)}, f32[512]{0:T(512)S(1)}) fusion(f32[512,4096]{1,0:T(8,128)S(1)} %get-tuple-element.25, f32[512]{0:T(512)S(1)} %get-tuple-element.23, s32[512]{0:T(512)S(1)} %broadcast_subtract_fusion), kind=kLoop, calls=%fused_computation.12 | loop fusion | flops 14679040 | bytes 8396800 | tf_op jit(solution)/shard_map/reduce_sum | solution.py:61
  55.1 0.7 broadcast_in_dim.34
  55.8 6.0 %all-to-all-start.1 = ((f32[32,2,512]{2,1,0:T(2,128)}), f32[32,2,512]{2,1,0:T(2,128)S(1)}, u32[]{:S(2)}, u32[]{:S(2)}) async-start(f32[32,2,512]{2,1,0:T(2,128)} %broadcast_in_dim.34), calls=%async_computation.1 | async-start | bytes 262144 | tf_op jit(solution)/shard_map/all_to_all | solution.py:32
  63.1 6.7 %all-to-all-done.1 = f32[32,2,512]{2,1,0:T(2,128)S(1)} async-done(((f32[32,2,512]{2,1,0:T(2,128)}), f32[32,2,512]{2,1,0:T(2,128)S(1)}, u32[]{:S(2)}, u32[]{:S(2)}) %all-to-all-start.1) | async-done | bytes 131104 | tf_op jit(solution)/shard_map/all_to_all | solution.py:32
  69.9 6.8 %multiply_convert_fusion = bf16[512,4096]{1,0:T(8,128)(2,1)S(1)} fusion(f32[512,4096]{1,0:T(8,128)} %copy-done.1, f32[512]{0:T(512)S(1)} %get-tuple-element.22, f32[512]{0:T(512)S(1)} %bitcast.83, f32[512]{0:T(512)S(1)} %get-tuple-element.23, s32[512]{0:T(512)S(1)} %broadcast_subtract_fusion), kind=kLoop, calls=%fused_computation.10 | loop fusion | flops 20971520 | bytes 12591104 | tf_op jit(solution)/shard_map/convert_element_type | solution.py:70
  76.7 3.2 %fusion.12 = bf16[512,512]{1,0:T(8,128)(2,1)} fusion(bf16[512,4096]{1,0:T(8,128)(2,1)S(1)} %multiply_convert_fusion, bf16[4096,512]{0,1:T(8,128)(2,1)S(1)} %copy-done, f32[4096]{0:T(1024)S(1)} %add_rsqrt_fusion), kind=kOutput, calls=%fused_computation.19 | convolution fusion | flops 2154037248 | bytes 8929280 | tf_op jit(solution)/shard_map/dot_general | solution.py:78
  79.9 2.6 %all-to-all-start.3 = ((bf16[32,16,512]{2,1,0:T(8,128)(2,1)}), bf16[32,16,512]{2,1,0:T(8,128)(2,1)S(1)}, u32[]{:S(2)}, u32[]{:S(2)}) async-start(bf16[32,16,512]{2,1,0:T(8,128)(2,1)} %bitcast.37), calls=%async_computation.3 | async-start | bytes 1048576 | tf_op jit(solution)/shard_map/all_to_all | solution.py:32
  85.2 12.9 %all-to-all-done.3 = bf16[32,16,512]{2,1,0:T(8,128)(2,1)S(1)} async-done(((bf16[32,16,512]{2,1,0:T(8,128)(2,1)}), bf16[32,16,512]{2,1,0:T(8,128)(2,1)S(1)}, u32[]{:S(2)}, u32[]{:S(2)}) %all-to-all-start.3) | async-done | bytes 524320 | tf_op jit(solution)/shard_map/all_to_all | solution.py:32
  98.1 2.9 %all-to-all-start.2 = ((bf16[32,16,392]{2,1,0:T(8,128)(2,1)}), bf16[32,16,392]{2,1,0:T(8,128)(2,1)S(1)}, u32[]{:S(2)}, u32[]{:S(2)}) async-start(bf16[32,16,392]{2,1,0:T(8,128)(2,1)} %constant_dynamic-update-slice_fusion), calls=%async_computation.2 | async-start | bytes 1048576 | tf_op jit(solution)/shard_map/all_to_all | solution.py:45
  101.0 9.5 %fusion.3 = (f32[4096]{0:T(1024)S(1)}, f32[4096,512]{0,1:T(8,128)}) fusion(bf16[4096,512]{0,1:T(8,128)(2,1)} %copy.49, f32[4096]{0:T(1024)S(1)} %add_rsqrt_fusion, bf16[512,4096]{1,0:T(8,128)(2,1)} %copy-done.2, bf16[512,512]{1,0:T(8,128)(2,1)S(1)} %fusion.15), kind=kOutput, calls=%fused_computation.5 | convolution fusion | flops 2155868160 | bytes 17334272 | tf_op jit(solution)/shard_map/dot_general | solution.py:71
  110.8 5.8 %all-to-all-done.2 = bf16[32,16,392]{2,1,0:T(8,128)(2,1)S(1)} async-done(((bf16[32,16,392]{2,1,0:T(8,128)(2,1)}), bf16[32,16,392]{2,1,0:T(8,128)(2,1)S(1)}, u32[]{:S(2)}, u32[]{:S(2)}) %all-to-all-start.2) | async-done | bytes 401440 | tf_op jit(solution)/shard_map/all_to_all | solution.py:45
  116.6 0.9 broadcast_in_dim.58
  117.5 3.0 %all-to-all-start.4 = ((bf16[32,16,512]{2,1,0:T(8,128)(2,1)}), bf16[32,16,512]{2,1,0:T(8,128)(2,1)S(1)}, u32[]{:S(2)}, u32[]{:S(2)}) async-start(bf16[32,16,512]{2,1,0:T(8,128)(2,1)} %broadcast_in_dim.58), calls=%async_computation.4 | async-start | bytes 1048576 | tf_op jit(solution)/shard_map/all_to_all | solution.py:32
  120.4 8.3 %fusion.6 = bf16[4096,512]{0,1:T(8,128)(2,1)} fusion(f32[4096,512]{0,1:T(8,128)} %get-tuple-element.27, bf16[4096,512]{0,1:T(8,128)(2,1)} %copy.49, f32[4096]{0:T(1024)S(1)} %get-tuple-element.26, f32[4096]{0:T(1024)S(1)} %add_rsqrt_fusion), kind=kLoop, calls=%fused_computation.8 | loop fusion | flops 12582912 | bytes 16809984 | tf_op jit(solution)/shard_map/convert_element_type | solution.py:77
  128.7 6.4 %copy.51 = bf16[4096,512]{1,0:T(8,128)(2,1)} copy(bf16[4096,512]{0,1:T(8,128)(2,1)} %fusion.6) | data formatting | bytes 8388608
  136.1 1.3 convolution_bitcast_fusion
  (58 shorter events, 22.6 us)
Async XLA Ops:
  0.6 14.9 %copy-start.3 = (bf16[16,12544]{1,0:T(8,128)(2,1)S(1)}, bf16[16,12544]{1,0:T(8,128)(2,1)}, u32[]{:S(2)}) copy-start(bf16[16,12544]{1,0:T(8,128)(2,1)} %param.4) | copy-start | bytes 1204228
  7.3 31.3 %copy-start.4 = (s32[512]{0:T(512)S(1)}, s32[512]{0:T(512)}, u32[]{:S(2)}) copy-start(s32[512]{0:T(512)} %param.7) | copy-start | bytes 6148
  8.2 34.2 %all-to-all-start = ((bf16[32,16,512]{2,1,0:T(8,128)(2,1)}), bf16[32,16,512]{2,1,0:T(8,128)(2,1)S(1)}, u32[]{:S(2)}, u32[]{:S(2)}) async-start(bf16[32,16,512]{2,1,0:T(8,128)(2,1)} %broadcast_in_dim.31), calls=%async_computation | async-start | bytes 1048576 | tf_op jit(solution)/shard_map/all_to_all | solution.py:32
  47.8 3.2 %copy-start.1 = (f32[512,4096]{1,0:T(8,128)}, f32[512,4096]{1,0:T(8,128)S(1)}, u32[]{:S(2)}) copy-start(f32[512,4096]{1,0:T(8,128)S(1)} %get-tuple-element.25) | copy-start | bytes 25165828
  55.8 14.0 %all-to-all-start.1 = ((f32[32,2,512]{2,1,0:T(2,128)}), f32[32,2,512]{2,1,0:T(2,128)S(1)}, u32[]{:S(2)}, u32[]{:S(2)}) async-start(f32[32,2,512]{2,1,0:T(2,128)} %broadcast_in_dim.34), calls=%async_computation.1 | async-start | bytes 262144 | tf_op jit(solution)/shard_map/all_to_all | solution.py:32
  69.9 6.8 %copy-start = (bf16[4096,512]{0,1:T(8,128)(2,1)S(1)}, bf16[4096,512]{0,1:T(8,128)(2,1)}, u32[]{:S(2)}) copy-start(bf16[4096,512]{0,1:T(8,128)(2,1)} %copy.49) | copy-start | bytes 12582916
  76.7 3.2 %copy-start.2 = (bf16[512,4096]{1,0:T(8,128)(2,1)}, bf16[512,4096]{1,0:T(8,128)(2,1)S(1)}, u32[]{:S(2)}) copy-start(bf16[512,4096]{1,0:T(8,128)(2,1)S(1)} %multiply_convert_fusion) | copy-start | bytes 12582916
  79.9 18.2 %all-to-all-start.3 = ((bf16[32,16,512]{2,1,0:T(8,128)(2,1)}), bf16[32,16,512]{2,1,0:T(8,128)(2,1)S(1)}, u32[]{:S(2)}, u32[]{:S(2)}) async-start(bf16[32,16,512]{2,1,0:T(8,128)(2,1)} %bitcast.37), calls=%async_computation.3 | async-start | bytes 1048576 | tf_op jit(solution)/shard_map/all_to_all | solution.py:32
  98.1 18.5 %all-to-all-start.2 = ((bf16[32,16,392]{2,1,0:T(8,128)(2,1)}), bf16[32,16,392]{2,1,0:T(8,128)(2,1)S(1)}, u32[]{:S(2)}, u32[]{:S(2)}) async-start(bf16[32,16,392]{2,1,0:T(8,128)(2,1)} %constant_dynamic-update-slice_fusion), calls=%async_computation.2 | async-start | bytes 1048576 | tf_op jit(solution)/shard_map/all_to_all | solution.py:45
  117.5 18.6 %all-to-all-start.4 = ((bf16[32,16,512]{2,1,0:T(8,128)(2,1)}), bf16[32,16,512]{2,1,0:T(8,128)(2,1)S(1)}, u32[]{:S(2)}, u32[]{:S(2)}) async-start(bf16[32,16,512]{2,1,0:T(8,128)(2,1)} %broadcast_in_dim.58), calls=%async_computation.4 | async-start | bytes 1048576 | tf_op jit(solution)/shard_map/all_to_all | solution.py:32
